TPU v7x, 512 devices: a whole 4x8x8 slice. The times are simulated.
512 devices in a mesh: dp: 8 (over z), vocab: 64 (over x, y, core).
Axes of the slice: x: 4, y: 8, z: 8, core: 2. Of those that a mesh axis runs over, the one named last changes fastest.
Arguments:
- pooled_grad: bfloat16 [16384, 1024], P(('dp', 'vocab')), may hold values from -12 to 12
- token_ids: int32 [16384, 16], P(('dp', 'vocab')), may hold values from 0 to 131071, as said below
Outputs:
- table_grad: float32 [131072, 1024], P(('dp', 'vocab'))
Inputs may be any that keep to these rules, and one draw needn't show every extreme that they name: `token_ids`: the owner of id r is (r // 256) % 64. Among the ids of one device's 32 positions at most 24 have the same owner; in every group of 64 devices along vocab some owner gets exactly 24 ids from each of them.
All inputs are finite; a program needn't handle non-finite values.
Results may differ from a plain program's by a relative error of at most 0.0075.
Values may be sent and summed in bfloat16 or wider, within the bound.
A program may use at most 64 MiB of HBM per device.

v0:
```python
import jax
import jax.numpy as jnp
from jax import lax
from jax.sharding import PartitionSpec as P

ROWS_DEV = 256
LIST = 16


def local(pooled_grad, token_ids):
    owners = lax.axis_size("vocab")
    positions = pooled_grad.shape[0]
    width = pooled_grad.shape[1]
    entries = positions * LIST
    capacity = entries * 3 // owners
    id_share = (pooled_grad.astype(jnp.float32) / LIST).astype(jnp.bfloat16)
    flat_ids = token_ids.reshape(-1)
    row_block = flat_ids // ROWS_DEV
    owner_of = row_block % owners
    column = row_block // owners * ROWS_DEV + flat_ids % ROWS_DEV
    member = (owner_of[:, None] == jnp.arange(owners, dtype=jnp.int32)[None, :]).astype(jnp.int32)
    earlier = jnp.cumsum(member, axis=0) - member
    within = jnp.sum(earlier * member, axis=1)
    slot_index = owner_of * capacity + within
    source = (
        jnp.zeros((owners * capacity,), jnp.int32)
        .at[slot_index]
        .set(jnp.arange(entries, dtype=jnp.int32))
    )
    filled = jnp.zeros((owners * capacity,), jnp.int32).at[slot_index].set(1)
    send_rows = id_share[source // LIST] * filled[:, None].astype(jnp.bfloat16)
    send_cols = jnp.where(filled > 0, column[source], -1)
    got_rows, got_cols = (
        lax.all_to_all(
            send_rows.reshape(owners, capacity, width),
            "vocab",
            split_axis=0,
            concat_axis=0,
            tiled=True,
        ),
        lax.all_to_all(
            send_cols.reshape(owners, capacity), "vocab", split_axis=0, concat_axis=0, tiled=True
        ),
    )
    got_rows = got_rows.reshape(owners * capacity, width)
    got_cols = got_cols.reshape(owners * capacity)
    wanted = jnp.arange(lax.axis_size("dp") * ROWS_DEV, dtype=jnp.int32)
    picker = (got_cols[None, :] == wanted[:, None]).astype(jnp.bfloat16)
    return lax.psum_scatter(
        jnp.dot(picker, got_rows, preferred_element_type=jnp.float32).astype(jnp.bfloat16),
        "dp",
        scatter_dimension=0,
        tiled=True,
    ).astype(jnp.float32)


def solution(mesh):
    in_specs = (P(("dp", "vocab"), None), P(("dp", "vocab"), None))
    out_specs = P(("dp", "vocab"), None)
    return jax.shard_map(local, mesh=mesh, in_specs=in_specs, out_specs=out_specs, check_vma=False)
```

profile of v0, /device:TPU:1, one launch (start us, length us, event | category | flops | bytes accessed | tf_op | source)
XLA Modules:
  0.0 202.6 jit_solution(15807797445018687574)
XLA Ops:
  6.5 0.8 copy.7
  7.3 0.1 reshape.178
  7.4 0.1 reshape.177
  7.5 0.1 reshape.176
  7.6 1.2 reduce-window.6
  8.8 0.2 slice_reduce_fusion
  9.1 0.1 fusion.5
  9.3 2.5 %scatter_custom_fusion.1 = s32[1536]{0:T(1024)S(1)} fusion(s32[512]{0:T(512)S(1)} %bitcast.30, s32[512]{0:T(512)S(1)} %iota.15, s32[]{:T(128)} %constant.66.clone.1), kind=kCustom, calls=%fused_computation.39 | custom fusion | bytes 6148 | tf_op jit(solution)/shard_map/scatter | solution.py:28
  11.7 2.5 %scatter_custom_fusion = s32[1536]{0:T(1024)S(1)} fusion(s32[512]{0:T(512)S(1)} %bitcast.31, s32[512]{0:T(512)S(1)} %ne.109, s32[]{:T(128)} %constant.66.clone.1), kind=kCustom, calls=%fused_computation.41 | custom fusion | bytes 6148 | tf_op jit(solution)/shard_map/scatter | solution.py:30
  14.2 0.0 copy-start
  14.2 9.5 %gather_fusion = s32[1536]{0:T(1024)S(1)} fusion(s32[512]{0:T(512)S(1)} %get-tuple-element.9, s32[2048]{0:T(1024)S(1)} %get-tuple-element.12), kind=kCustom, calls=%fused_computation | custom fusion | bytes 18432 | tf_op jit(solution)/shard_map/gather | solution.py:32
  23.7 0.7 all_to_all.9
  24.4 11.6 %all-to-all-start = ((s32[64,1,24]{2,1,0:T(1,128)}), s32[64,1,24]{2,1,0:T(1,128)S(1)}, u32[]{:S(2)}, u32[]{:S(2)}) async-start(s32[64,1,24]{2,1,0:T(1,128)} %bitcast.3), calls=%async_computation | async-start | bytes 65536 | tf_op jit(solution)/shard_map/all_to_all | solution.py:41
  36.1 0.0 copy-done
  36.1 0.1 mul.35
  36.2 5.1 %gather_fusion.1 = bf16[1536,1024]{1,0:T(8,128)(2,1)S(1)} fusion(bf16[32,1024]{1,0:T(8,128)(2,1)S(1)} %multiply_convert_fusion, s32[2048]{0:T(1024)S(1)} %get-tuple-element.11), kind=kCustom, calls=%fused_computation.1 | custom fusion | bytes 6297600 | tf_op jit(solution)/shard_map/gather | solution.py:31
  41.3 1.9 broadcast_multiply_fusion
  43.2 2.1 %all-to-all-done = s32[64,1,24]{2,1,0:T(1,128)S(1)} async-done(((s32[64,1,24]{2,1,0:T(1,128)}), s32[64,1,24]{2,1,0:T(1,128)S(1)}, u32[]{:S(2)}, u32[]{:S(2)}) %all-to-all-start) | async-done | bytes 6176 | tf_op jit(solution)/shard_map/all_to_all | solution.py:41
  45.3 8.2 %all-to-all-start.1 = ((bf16[64,24,1024]{2,1,0:T(8,128)(2,1)}), bf16[64,24,1024]{2,1,0:T(8,128)(2,1)S(1)}, u32[]{:S(2)}, u32[]{:S(2)}) async-start(bf16[64,24,1024]{2,1,0:T(8,128)(2,1)} %broadcast_multiply_fusion), calls=%async_computation.1 | async-start | bytes 6291456 | tf_op jit(solution)/shard_map/all_to_all | solution.py:34
  53.5 0.0 reduce-scatter.2.cloned.1.call-start
  53.6 0.5 broadcast.271
  54.1 0.7 reduce.5
  54.8 0.1 eq.45
  54.9 72.1 %all-to-all-done.1 = bf16[64,24,1024]{2,1,0:T(8,128)(2,1)S(1)} async-done(((bf16[64,24,1024]{2,1,0:T(8,128)(2,1)}), bf16[64,24,1024]{2,1,0:T(8,128)(2,1)S(1)}, u32[]{:S(2)}, u32[]{:S(2)}) %all-to-all-start.1) | async-done | bytes 3145760 | tf_op jit(solution)/shard_map/all_to_all | solution.py:34
  127.0 8.1 %fusion.2 = bf16[2048,1024]{1,0:T(8,128)(2,1)} fusion(bf16[1536,1024]{1,0:T(8,128)(2,1)S(1)} %bitcast.28, s32[1536]{0:T(1024)S(1)} %eq.45), kind=kOutput, calls=%fused_computation.7 | convolution fusion | flops 6447693824 | bytes 7346176 | tf_op jit(solution)/shard_map/dot_general | solution.py:50
  135.1 0.0 reduce-scatter.2.cloned.1.call-update
  135.2 58.5 %reduce-scatter.2.cloned.1.call-done = bf16[256,1024]{1,0:T(8,128)(2,1)} async-done(((bf16[2048,1024]{1,0:T(8,128)(2,1)}), bf16[256,1024]{1,0:T(8,128)(2,1)}) %reduce-scatter.2.cloned.1.call-update) | async-done | bytes 524304 | tf_op jit(solution)/shard_map/reduce_scatter | solution.py:49
  193.7 2.1 %convert_element_type.30 = f32[256,1024]{1,0:T(8,128)} convert(bf16[256,1024]{1,0:T(8,128)(2,1)} %reduce-scatter.2.cloned.1.call-done) | non-fusion elementwise | flops 262144 | bytes 1572864 | tf_op jit(solution)/shard_map/convert_element_type | solution.py:54
  (12 shorter events, 0.2 us)
Async XLA Ops:
  14.2 21.8 %copy-start = (bf16[32,1024]{1,0:T(8,128)(2,1)S(1)}, bf16[32,1024]{1,0:T(8,128)(2,1)}, u32[]{:S(2)}) copy-start(bf16[32,1024]{1,0:T(8,128)(2,1)} %param.2) | copy-start | bytes 196612
  24.4 20.9 %all-to-all-start = ((s32[64,1,24]{2,1,0:T(1,128)}), s32[64,1,24]{2,1,0:T(1,128)S(1)}, u32[]{:S(2)}, u32[]{:S(2)}) async-start(s32[64,1,24]{2,1,0:T(1,128)} %bitcast.3), calls=%async_computation | async-start | bytes 65536 | tf_op jit(solution)/shard_map/all_to_all | solution.py:41
  45.3 81.7 %all-to-all-start.1 = ((bf16[64,24,1024]{2,1,0:T(8,128)(2,1)}), bf16[64,24,1024]{2,1,0:T(8,128)(2,1)S(1)}, u32[]{:S(2)}, u32[]{:S(2)}) async-start(bf16[64,24,1024]{2,1,0:T(8,128)(2,1)} %broadcast_multiply_fusion), calls=%async_computation.1 | async-start | bytes 6291456 | tf_op jit(solution)/shard_map/all_to_all | solution.py:34
  53.5 140.1 %reduce-scatter.2.cloned.1.call-start = ((), (), s32[]{:S(2)}) async-start(), calls=%async_computation.3 | async-start | bytes 4718592 | tf_op jit(solution)/shard_map/reduce_scatter | solution.py:49
Sparse Core Ops, SparseCore 0:
  135.3 58.3 reduce-scatter.1
where the time goes:
time: 203 us
  waiting for transfers between devices  133 us (66%)
  local copies, waits for them, and re-layouts  22.1 us (11%)
  starting transfers between devices  19.9 us (10%)
  between operations  13.6 us (7%)
  matrix products  8.13 us (4%)
  other arithmetic  6.28 us (3%)
    all_to_all x1, waiting for transfers between devices, local(): lax.all_to_all(send_rows.reshape(owners, capacity, width), 'vocab', split...  72.1 us
    reduce_scatter x1, waiting for transfers between devices, local(): lax.psum_scatter(jnp.dot(picker, got_rows, preferred_element_type=jnp.flo...  58.5 us
    all_to_all x1, starting transfers between devices, local(): lax.all_to_all(send_cols.reshape(owners, capacity), 'vocab', split_axis=0...  11.6 us
    gather x1, local copies, waits for them, and re-layouts, local(): send_cols = jnp.where(filled > 0, column[source], -1)  9.48 us
    all_to_all x1, starting transfers between devices, local(): lax.all_to_all(send_rows.reshape(owners, capacity, width), 'vocab', split...  8.24 us
    dot_general x1, matrix products, local(): jnp.dot(picker, got_rows, preferred_element_type=jnp.float32)  8.13 us
    gather x1, local copies, waits for them, and re-layouts, local(): send_rows = id_share[source // LIST] * filled[:, None].astype(jnp.bfloat16)  5.07 us
  transfers between devices with their start and end apart: 3, of which 3 were waited for; matrix products, arithmetic and copies ran while one was open for 4% of the time, Pallas kernels for 0%

commit v1 on v0

v1 whole, which is shorter than its diff:
```python
import functools

import jax
import jax.numpy as jnp
from jax import lax
from jax.experimental import pallas as pl
from jax.experimental.pallas import tpu as pltpu
from jax.sharding import PartitionSpec as P

ROWS = 256
LIST = 16
CH = 256
HALF = CH // 2
MESH = pl.DeviceIdType.MESH
MSG = ((4, 0), (3, 1), (3, 0), (2, 1), (2, 0), (1, 1), (1, 0))


def kernel(
    nx, ny, nc, x_hbm, ids_hbm, out_ref,
    x_in, ids_in, xg, ids_x, ids_g, cnt, part, send, got,
    in_sem, id1_s, id1_r, id2_s, id2_r, id3_s, id3_r,
    a1_s, a1_r, b1_s, b1_r, a2_s, a2_r, b2_s, b2_r, p_s, p_r, z_s, z_r,
):
    d = lax.axis_index("dp")
    v = lax.axis_index("vocab")
    c = v % 2
    y = (v // 2) % ny
    x = v // (2 * ny)

    def at(xx, yy, cc):
        return (d, (xx * ny + yy) * 2 + cc)

    xs = [lax.rem(x + k, nx) for k in range(nx)]
    ys = [lax.rem(y + k, ny) for k in range(ny)]
    other = 1 - c
    down = (lax.rem(d + 7, 8), v)
    up = (lax.rem(d + 1, 8), v)

    cp_ids = pltpu.make_async_copy(ids_hbm, ids_in, in_sem.at[0])
    cp_x = pltpu.make_async_copy(x_hbm, x_in, in_sem.at[1])
    cp_ids.start()
    cp_x.start()

    peers = [at(xs[k], y, c) for k in range(1, nx)] + [at(x, ys[k], c) for k in range(1, ny)]
    peers += [at(x, y, other), down, up]
    barrier = pltpu.get_barrier_semaphore()
    for peer in peers:
        pl.semaphore_signal(barrier, inc=1, device_id=peer, device_id_type=MESH)
    cp_ids.wait()
    cp_x.wait()
    for f in range(nc):
        for h in range(2):
            xg[f, c, y, x, h] = x_in[pl.ds(16 * h, 16), pl.ds(CH * f, CH)]
    ids_x[x] = ids_in[...]
    pl.semaphore_wait(barrier, len(peers))

    def rc(src, dst, ss, rs, dev):
        return pltpu.make_async_remote_copy(
            src_ref=src, dst_ref=dst, send_sem=ss, recv_sem=rs, device_id=dev, device_id_type=MESH
        )

    def first(f):
        lanes = pl.ds(CH * f, CH)
        r = []
        for k in range(1, ny):
            r.append(
                rc(x_in.at[pl.ds(16, 16), lanes], xg.at[f, c, y, x, 1], b1_s.at[f, k], b1_r.at[f, k], at(x, ys[k], c))
            )
        for k in range(1, nx):
            r.append(
                rc(x_in.at[pl.ds(0, 16), lanes], xg.at[f, c, y, x, 0], a1_s.at[f, k], a1_r.at[f, k], at(xs[k], y, c))
            )
        return r

    def second(f):
        a = [
            rc(xg.at[f, c, y, :, 0], xg.at[f, c, y, :, 0], a2_s.at[f, k], a2_r.at[f, k], at(x, ys[k], c))
            for k in range(1, ny)
        ]
        b = [
            rc(xg.at[f, c, :, x, 1], xg.at[f, c, :, x, 1], b2_s.at[f, k], b2_r.at[f, k], at(xs[k], y, c))
            for k in range(1, nx)
        ]
        return a, b

    def third(f):
        return rc(xg.at[f, c], xg.at[f, c], p_s.at[f], p_r.at[f], at(x, y, other))

    def start(copies):
        for cp in copies:
            cp.start()

    def arrived(copies):
        for cp in copies:
            cp.wait_recv()

    def sent(copies):
        for cp in copies:
            cp.wait_send()

    def go_second(f):
        arrived(first(f))
        a, b = second(f)
        start(a)
        start(b)

    def go_third(f):
        a, b = second(f)
        arrived(a)
        arrived(b)
        third(f).start()

    id1 = [rc(ids_in, ids_x.at[x], id1_s.at[k], id1_r.at[k], at(xs[k], y, c)) for k in range(1, nx)]
    id2 = [rc(ids_g.at[c, y], ids_g.at[c, y], id2_s.at[k], id2_r.at[k], at(x, ys[k], c)) for k in range(1, ny)]
    id3 = rc(ids_g.at[c], ids_g.at[c], id3_s, id3_r, at(x, y, other))

    start(id1)
    start(first(0))
    arrived(id1)
    lane = lax.broadcasted_iota(jnp.int32, (LIST, 128), 1) // 32
    both = ids_x[0]
    for k in range(1, nx):
        both = jnp.where(lane == k, ids_x[k], both)
    ids_g[c, y] = both
    start(id2)
    go_second(0)
    if nc > 1:
        start(first(1))
    arrived(id2)
    id3.start()
    id3.wait_recv()

    blocks = [lax.rem(d + k, 8) for k in (4, 5, 3, 6, 2, 7, 1, 0)]
    kt = 2 * ny
    row = lax.broadcasted_iota(jnp.int32, (ROWS, 128), 0).astype(jnp.float32).astype(jnp.bfloat16)
    one = jnp.full((ROWS, 128), 1.0 / LIST, jnp.bfloat16)
    zero = jnp.zeros((ROWS, 128), jnp.bfloat16)

    def build(i):
        block = blocks[i]

        def tile(t, _):
            ids = ids_g[t // ny, t % ny]
            hit = (ids // ROWS) == block * (2 * nx * ny) + v
            low = jnp.where(hit, ids % ROWS, -1).astype(jnp.float32).astype(jnp.bfloat16)
            acc = zero
            for j in range(LIST):
                acc = acc + jnp.where(jnp.broadcast_to(low[j : j + 1], (ROWS, 128)) == row, one, zero)
            cnt[i, :, pl.ds(pl.multiple_of(t * 128, 128), 128)] = acc
            return 0

        lax.fori_loop(0, kt, tile, 0)

    def dot(i, f):
        part[i] = jnp.dot(
            cnt[i], xg[f].reshape(kt * 128, CH), preferred_element_type=jnp.float32
        )

    build(0)
    go_third(0)
    build(1)
    build(2)
    third(0).wait_recv()

    def zcopy(way, f, m):
        return rc(
            send.at[way, f, m], got.at[way, f, m], z_s.at[way, f, m], z_r.at[way, f, m], (down, up)[way]
        )

    def part_of(way, m):
        dist, half = MSG[m]
        if way == 1:
            half = 1 - half
        i = 0 if dist == 4 else 2 * (4 - dist) - 1 + way
        return part[i, :, HALF * half : HALF * (half + 1)]

    def finish(f):
        lanes0 = CH * f
        for way in range(2):
            for m in (5, 6):
                zcopy(way, f, m).wait_recv()
        lo = part[7, :, :HALF] + got[0, f, 6].astype(jnp.float32) + got[1, f, 5].astype(jnp.float32)
        hi = part[7, :, HALF:] + got[0, f, 5].astype(jnp.float32) + got[1, f, 6].astype(jnp.float32)
        out_ref[:, pl.ds(pl.multiple_of(lanes0, 128), HALF)] = lo
        out_ref[:, pl.ds(pl.multiple_of(lanes0 + HALF, 128), HALF)] = hi

    def chunk(f, _):
        @pl.when(f > 0)
        def _():
            third(f).wait_recv()

        for i in range(3):
            dot(i, f)
        for m in range(2):
            for way in range(2):
                send[way, f, m] = part_of(way, m).astype(jnp.bfloat16)
                zcopy(way, f, m).start()

        @pl.when(f > 0)
        def _():
            finish(f - 1)

        @pl.when(f + 1 < nc)
        def _():
            go_second(f + 1)

        @pl.when(f + 2 < nc)
        def _():
            start(first(f + 2))

        for i in range(3, 8):
            @pl.when(f == 0)
            def _(i=i):
                build(i)

            dot(i, f)
            if i in (4, 6):
                for m in ((2, 3) if i == 4 else (4,)):
                    for way in range(2):
                        zcopy(way, f, m - 2).wait_recv()
                        send[way, f, m] = (
                            part_of(way, m) + got[way, f, m - 2].astype(jnp.float32)
                        ).astype(jnp.bfloat16)
                        zcopy(way, f, m).start()

        @pl.when(f + 1 < nc)
        def _():
            go_third(f + 1)

        for m in (5, 6):
            for way in range(2):
                zcopy(way, f, m - 2).wait_recv()
                send[way, f, m] = (part_of(way, m) + got[way, f, m - 2].astype(jnp.float32)).astype(
                    jnp.bfloat16
                )
                zcopy(way, f, m).start()
        return 0

    lax.fori_loop(0, nc, chunk, 0)
    finish(nc - 1)

    sent(id1)
    sent(id2)
    id3.wait_send()

    def drain(f, _):
        sent(first(f))
        a, b = second(f)
        sent(a)
        sent(b)
        third(f).wait_send()
        for way in range(2):
            for m in range(7):
                zcopy(way, f, m).wait_send()
        return 0

    lax.fori_loop(0, nc, drain, 0)


def local(nx, ny, pooled_grad, token_ids):
    width = pooled_grad.shape[1]
    nc = width // CH
    ids = jnp.tile(token_ids.T, (1, 4))
    dma = pltpu.SemaphoreType.DMA
    bf = jnp.bfloat16
    return pl.pallas_call(
        functools.partial(kernel, nx, ny, nc),
        out_shape=jax.ShapeDtypeStruct((ROWS, width), jnp.float32),
        in_specs=[pl.BlockSpec(memory_space=pl.ANY)] * 2,
        out_specs=pl.BlockSpec(memory_space=pltpu.VMEM),
        scratch_shapes=[
            pltpu.VMEM((32, width), bf),
            pltpu.VMEM((LIST, 128), jnp.int32),
            pltpu.VMEM((nc, 2, ny, nx, 2, 16, CH), bf),
            pltpu.VMEM((nx, LIST, 128), jnp.int32),
            pltpu.VMEM((2, ny, LIST, 128), jnp.int32),
            pltpu.VMEM((8, ROWS, 2 * ny * 128), bf),
            pltpu.VMEM((8, ROWS, CH), jnp.float32),
            pltpu.VMEM((2, nc, 7, ROWS, HALF), bf),
            pltpu.VMEM((2, nc, 7, ROWS, HALF), bf),
            dma((2,)),
            dma((nx,)), dma((nx,)), dma((ny,)), dma((ny,)), dma, dma,
            dma((nc, nx)), dma((nc, nx)), dma((nc, ny)), dma((nc, ny)),
            dma((nc, ny)), dma((nc, ny)), dma((nc, nx)), dma((nc, nx)),
            dma((nc,)), dma((nc,)), dma((2, nc, 7)), dma((2, nc, 7)),
        ],
        compiler_params=pltpu.CompilerParams(
            collective_id=0, has_side_effects=True, vmem_limit_bytes=60 * 1024 * 1024
        ),
    )(pooled_grad, ids)


def solution(mesh, nx=4, ny=8):
    in_specs = (P(("dp", "vocab"), None), P(("dp", "vocab"), None))
    out_specs = P(("dp", "vocab"), None)
    return jax.shard_map(
        functools.partial(local, nx, ny), mesh=mesh, in_specs=in_specs, out_specs=out_specs, check_vma=False
    )
```

time: 203 us -> 102 us (0.50)
  waiting for transfers between devices: 133 us -> 0 us
  Pallas kernels: 0 us -> 97.3 us
  starting transfers between devices: 19.9 us -> 0 us
  local copies, waits for them, and re-layouts: 22.1 us -> 3.69 us
  between operations: 13.6 us -> 0.01 us
  matrix products: 8.13 us -> 0 us
  other arithmetic: 6.28 us -> 0 us
    pallas_call x0 -> x1, Pallas kernels: none -> 97.3 us  [local(): pl.pallas_call(functools.partial(kernel, nx, ny, nc), out_shape=jax.Shape...]
    all_to_all x2 -> x0, waiting for transfers between devices: 74.2 us -> none  [the longest x1 72.1 us: local(): lax.all_to_all(send_rows.reshape(owners, capacity, width), 'vocab', split...]
    reduce_scatter x1 -> x0, waiting for transfers between devices: 58.5 us -> none  [local(): lax.psum_scatter(jnp.dot(picker, got_rows, preferred_element_type=jnp.flo...]
    all_to_all x2 -> x0, starting transfers between devices: 19.8 us -> none  [the longest x1 11.6 us: local(): lax.all_to_all(send_cols.reshape(owners, capacity), 'vocab', split_axis=0...]
    gather x2 -> x0, local copies, waits for them, and re-layouts: 14.6 us -> none  [the longest x1 9.48 us: local(): send_cols = jnp.where(filled > 0, column[source], -1)]
    dot_general x1 -> x0, matrix products: 8.13 us -> none  [local(): jnp.dot(picker, got_rows, preferred_element_type=jnp.float32)]
    scatter x2 -> x0, local copies, waits for them, and re-layouts: 4.9 us -> none  [the longest x1 2.45 us: local(): source = jnp.zeros((owners * capacity,), jnp.int32).at[slot_index].set(jn...]
    convert_element_type x3 -> x0, other arithmetic: 2.15 us -> none  [the longest x1 2.13 us: local(): return lax.psum_scatter(jnp.dot(picker, got_rows, preferred_element_type=...]
  transfers between devices with their start and end apart: 3 -> 0, of which waited for: 3 -> 0; matrix products, arithmetic and copies ran while one was open for 4% -> 0% of each run, Pallas kernels for 0% -> 0%
where the time goes in v1:
time: 102 us; the launch traced here: 101 us
  Pallas kernels  97.3 us (95%)
  local copies, waits for them, and re-layouts  3.69 us (4%)
    pallas_call x1, Pallas kernels, local(): pl.pallas_call(functools.partial(kernel, nx, ny, nc), out_shape=jax.Shape...  97.3 us
    unnamed x1, local copies, waits for them, and re-layouts  2.31 us

profile of v1, /device:TPU:1, one launch (start us, length us, event | category | flops | bytes accessed | tf_op | source)
XLA Modules:
  0.0 101.0 jit_solution(16925591277108170073)
XLA Ops:
  0.0 0.7 tile.4
  0.7 0.7 tile.10.ids_hbm
  1.4 97.3 %shard_map.28 = f32[256,1024]{1,0:T(8,128)} custom-call(bf16[32,1024]{1,0:T(8,128)(2,1)} %x_hbm.1, s32[16,128]{1,0:T(8,128)} %tile.10.ids_hbm), custom_call_target="tpu_custom_call" | custom-call | tf_op jit(solution)/shard_map/pallas_call | solution.py:266
  98.7 2.3 %copy.4 = f32[256,1024]{1,0:T(8,128)} copy(f32[256,1024]{1,0:T(8,128)} %shard_map.28) | data formatting | bytes 2097152

commit v2 on v0

v2 whole, which is shorter than its diff:
```python
import functools

import jax
import jax.numpy as jnp
from jax import lax
from jax.experimental import pallas as pl
from jax.experimental.pallas import tpu as pltpu
from jax.sharding import PartitionSpec as P

ROWS = 256
HALF = ROWS // 2
LIST = 16
POS = 32
WIDTHS = (128, 256, 256, 256, 128)
OFFS = tuple(sum(WIDTHS[:i]) for i in range(len(WIDTHS)))
NC = len(WIDTHS)
MESH = pl.DeviceIdType.MESH
MSG = ((4, 0), (3, 1), (3, 0), (2, 1), (2, 0), (1, 1), (1, 0))
ROUNDS = ((0, 1), (2, 3), (4, 5), (6,))
BLOCKS = (4, 5, 3, 6, 2, 7, 1, 0)
GROUPS = ((0, 3), (3, 5), (5, 8), (3, 8), (0, 8))


def kernel(nx, ny, x_hbm, ids_hbm, out_hbm, x_in, ids_in, ids_x, ids_g, cnt, *rest):
    xg, part, send, got, outs = (rest[NC * i : NC * (i + 1)] for i in range(5))
    in_sem, out_sem, id_s, id_r, g_s, g_r, z_s, z_r = rest[5 * NC :]
    scope = jax.named_scope
    d = lax.axis_index("dp")
    v = lax.axis_index("vocab")
    c = v % 2
    y = (v // 2) % ny
    x = v // (2 * ny)

    def at(xx, yy, cc):
        return (d, (xx * ny + yy) * 2 + cc)

    xs = [lax.rem(x + k, nx) for k in range(nx)]
    ys = [lax.rem(y + k, ny) for k in range(ny)]
    partner = at(x, y, 1 - c)
    down = (lax.rem(d + 7, 8), v)
    up = (lax.rem(d + 1, 8), v)

    cp_ids = pltpu.make_async_copy(ids_hbm, ids_in, in_sem.at[0])
    cp_x = pltpu.make_async_copy(x_hbm, x_in, in_sem.at[1])
    cp_ids.start()
    cp_x.start()

    peers = [at(x, ys[k], c) for k in range(1, ny)] + [at(xs[k], y, c) for k in range(1, nx)]
    peers += [partner, down, up]
    barrier = pltpu.get_barrier_semaphore()
    for peer in peers:
        pl.semaphore_signal(barrier, inc=1, device_id=peer, device_id_type=MESH)
    cp_ids.wait()
    ids_x[x] = jnp.concatenate([ids_in[...]] * nx, axis=1)
    cp_x.wait()
    for f in range(NC):
        xg[f][c, y, x] = x_in[:, pl.ds(OFFS[f], WIDTHS[f])]
    with scope("barrier"):
        pl.semaphore_wait(barrier, len(peers))

    def rc(src, dst, ss, rs, dev):
        return pltpu.make_async_remote_copy(
            src_ref=src, dst_ref=dst, send_sem=ss, recv_sem=rs, device_id=dev, device_id_type=MESH
        )

    def start(copies):
        for cp in copies:
            cp.start()

    def whole(ref, sems, at_):
        return rc(ref, ref, sems[0].at[*at_], sems[1].at[*at_], partner)

    gs = (g_s, g_r)

    def along_y(f):
        src = x_in.at[:, pl.ds(OFFS[f], WIDTHS[f])]
        return [
            rc(src, xg[f].at[c, y, x], g_s.at[f, 0], g_r.at[f, 0], at(x, ys[k], c)) for k in range(1, ny)
        ]

    def along_x(f):
        ref = xg[f].at[c, :, x]
        return [rc(ref, ref, g_s.at[f, 1], g_r.at[f, 1], at(xs[k], y, c)) for k in (1, nx - 1)]

    def relay(f):
        lo = xg[f].at[c, pl.ds(0, ny // 2), xs[nx - 1]]
        hi = xg[f].at[c, pl.ds(ny // 2, ny // 2), xs[1]]
        return [
            rc(lo, lo, g_s.at[f, 2], g_r.at[f, 2], at(xs[1], y, c)),
            rc(hi, hi, g_s.at[f, 2], g_r.at[f, 2], at(xs[nx - 1], y, c)),
        ]

    def across(f, k):
        ref = xg[f].at[c, :, xs[k]]
        return rc(ref, ref, g_s.at[f, 3], g_r.at[f, 3], partner)

    def all_of(f, step):
        ref = (
            xg[f].at[c, pl.ds(0, ny - 1), 0],
            xg[f].at[c, :, pl.ds(0, 2)],
            xg[f].at[c, :, 0],
            xg[f].at[c],
        )[step]
        return whole(ref, gs, (f, step))

    def gather1(f):
        start(along_y(f))

    def gather2(f):
        with scope(f"g2_{f}"):
            all_of(f, 0).wait_recv()
        start(along_x(f))
        across(f, 0).start()

    def gather3(f):
        with scope(f"g3_{f}"):
            all_of(f, 1).wait_recv()
        start(relay(f))
        across(f, 1).start()
        across(f, nx - 1).start()

    def gather4(f):
        with scope(f"g4_{f}"):
            all_of(f, 2).wait_recv()
        across(f, 2).start()

    def gather5(f):
        with scope(f"g5_{f}"):
            all_of(f, 3).wait_recv()

    id1 = [rc(ids_x.at[x], ids_x.at[x], id_s.at[0], id_r.at[0], at(xs[k], y, c)) for k in range(1, nx)]
    id2 = [rc(ids_g.at[c, y], ids_g.at[c, y], id_s.at[1], id_r.at[1], at(x, ys[k], c)) for k in range(1, ny)]
    id3 = rc(ids_g.at[c], ids_g.at[c], id_s.at[2], id_r.at[2], partner)
    id1_all = whole(ids_x.at[pl.ds(0, nx - 1)], (id_s, id_r), (0,))
    id2_all = whole(ids_g.at[c, pl.ds(0, ny - 1)], (id_s, id_r), (1,))

    blocks = [lax.rem(d + k, 8) for k in BLOCKS]
    kt = 2 * ny

    def build(g, core):
        lo, hi = GROUPS[g]

        def tile(k, _):
            ids = ids_g[core, k]
            t = core * ny + k
            low = ids & (ROWS - 1)
            block = ids >> 8
            word = low & 31
            bit = jnp.left_shift(1, (low >> 5) * 4)
            wide = lax.broadcasted_iota(jnp.int32, (32, 128), 0)
            vals = [jnp.where(block == blocks[i] * (2 * nx * ny) + v, bit, 0) for i in range(lo, hi)]
            acc = [[jnp.zeros((32, 128), jnp.int32) for _ in range(2)] for _ in vals]
            for j in range(LIST):
                eq = jnp.broadcast_to(word[j : j + 1], (32, 128)) == wide
                for n, val in enumerate(vals):
                    acc[n][j // 8] += jnp.where(eq, jnp.broadcast_to(val[j : j + 1], (32, 128)), 0)
            nib = 0x0F0F0F0F
            for n in range(len(vals)):
                a, b = acc[n]
                both = ((a & nib) + (b & nib), ((a >> 4) & nib) + ((b >> 4) & nib))
                for s in range(8):
                    count = (both[s % 2] >> (8 * (s // 2))) & 255
                    cnt[lo + n, pl.ds(32 * s, 32), pl.ds(pl.multiple_of(t * 128, 128), 128)] = count.astype(
                        jnp.float32
                    ).astype(jnp.bfloat16)
            return 0

        with scope(f"build{g}"):
            lax.fori_loop(0, ny, tile, 0)

    def dots(f, g):
        lo, hi = GROUPS[g]
        with scope(f"dot{f}{g}"):
            part[f][lo:hi] = jnp.dot(
                cnt[lo:hi].reshape((hi - lo) * ROWS, kt * 128),
                xg[f][...].reshape(kt * 128, WIDTHS[f]),
                preferred_element_type=jnp.float32,
            ).reshape(hi - lo, ROWS, WIDTHS[f])

    def zcopy(way, f, m):
        return rc(
            send[f].at[way, m], got[f].at[way, m], z_s.at[f], z_r.at[f, way, m], (down, up)[way]
        )

    def reduce(f, r):
        for m in ROUNDS[r]:
            for way in range(2):
                dist, half = MSG[m]
                half = half if way == 0 else 1 - half
                i = 0 if dist == 4 else 2 * (4 - dist) - 1 + way
                value = part[f][i, HALF * half : HALF * (half + 1)]
                if m >= 2:
                    with scope(f"w{f}{m - 2}"):
                        zcopy(way, f, m - 2).wait_recv()
                    value = value + got[f][way, m - 2].astype(jnp.float32)
                send[f][way, m] = value.astype(jnp.bfloat16)
                zcopy(way, f, m).start()

    def put(f):
        return pltpu.make_async_copy(outs[f], out_hbm.at[:, pl.ds(OFFS[f], WIDTHS[f])], out_sem.at[f])

    def finish(f):
        with scope(f"fin{f}"):
            for m in (5, 6):
                for way in range(2):
                    zcopy(way, f, m).wait_recv()
        for half in range(2):
            rows = slice(HALF * half, HALF * (half + 1))
            total = part[f][7, rows] + (
                got[f][0, 6 - half].astype(jnp.float32) + got[f][1, 5 + half].astype(jnp.float32)
            )
            outs[f][rows] = total * (1.0 / LIST)
        put(f).start()

    start(id1)
    gather1(0)
    with scope("id1"):
        id1_all.wait_recv()
    lane = lax.broadcasted_iota(jnp.int32, (LIST, 128), 1) // POS
    both = ids_x[0]
    for k in range(1, nx):
        both = jnp.where(lane == k, ids_x[k], both)
    ids_g[c, y] = both
    start(id2)
    gather1(1)
    gather2(0)
    with scope("id2"):
        id2_all.wait_recv()
    id3.start()
    build(0, c)
    gather3(0)
    with scope("id3"):
        id3.wait_recv()
    build(0, 1 - c)
    gather2(1)
    gather1(2)
    build(1, c)
    gather4(0)
    build(1, 1 - c)
    gather5(0)
    dots(0, 0)
    reduce(0, 0)
    gather3(1)
    dots(0, 1)
    build(2, c)
    gather2(2)
    gather1(3)
    build(2, 1 - c)
    gather4(1)
    reduce(0, 1)
    gather5(1)
    dots(1, 0)
    reduce(1, 0)
    gather3(2)
    dots(0, 2)
    reduce(0, 2)
    dots(1, 3)
    gather4(2)
    gather2(3)
    gather1(4)
    reduce(1, 1)
    gather5(2)
    dots(2, 0)
    reduce(2, 0)
    reduce(0, 3)
    dots(2, 3)
    gather3(3)
    reduce(1, 2)
    reduce(2, 1)
    gather2(4)
    finish(0)
    gather4(3)
    gather5(3)
    dots(3, 0)
    reduce(3, 0)
    reduce(1, 3)
    dots(3, 3)
    reduce(2, 2)
    gather3(4)
    reduce(3, 1)
    finish(1)
    gather4(4)
    gather5(4)
    dots(4, 4)
    reduce(4, 0)
    reduce(2, 3)
    reduce(3, 2)
    reduce(4, 1)
    finish(2)
    reduce(3, 3)
    reduce(4, 2)
    finish(3)
    reduce(4, 3)
    finish(4)

    with scope("drain"):
        id1_all.wait_send()
        id2_all.wait_send()
        id3.wait_send()
        for f in range(NC):
            for step in range(4):
                all_of(f, step).wait_send()
            rc(send[f], send[f], z_s.at[f], z_r.at[f, 0, 0], down).wait_send()
            put(f).wait()


def local(nx, ny, pooled_grad, token_ids):
    width = pooled_grad.shape[1]
    dma = pltpu.SemaphoreType.DMA
    bf = jnp.bfloat16
    vmem = pltpu.VMEM
    return pl.pallas_call(
        functools.partial(kernel, nx, ny),
        out_shape=jax.ShapeDtypeStruct((ROWS, width), jnp.float32),
        in_specs=[pl.BlockSpec(memory_space=pl.ANY)] * 2,
        out_specs=pl.BlockSpec(memory_space=pl.ANY),
        scratch_shapes=[
            vmem((POS, width), bf),
            vmem((LIST, POS), jnp.int32),
            vmem((nx, LIST, 128), jnp.int32),
            vmem((2, ny, LIST, 128), jnp.int32),
            vmem((8, ROWS, 2 * ny * 128), bf),
            *[vmem((2, ny, nx, POS, w), bf) for w in WIDTHS],
            *[vmem((8, ROWS, w), jnp.float32) for w in WIDTHS],
            *[vmem((2, 7, HALF, w), bf) for w in WIDTHS],
            *[vmem((2, 7, HALF, w), bf) for w in WIDTHS],
            *[vmem((ROWS, w), jnp.float32) for w in WIDTHS],
            dma((2,)), dma((NC,)), dma((3,)), dma((3,)),
            dma((NC, 4)), dma((NC, 4)), dma((NC,)), dma((NC, 2, 7)),
        ],
        compiler_params=pltpu.CompilerParams(
            collective_id=0, has_side_effects=True, vmem_limit_bytes=62 * 1024 * 1024
        ),
    )(pooled_grad, token_ids.T)


def solution(mesh, nx=4, ny=8):
    in_specs = (P(("dp", "vocab"), None), P(("dp", "vocab"), None))
    out_specs = P(("dp", "vocab"), None)
    return jax.shard_map(
        functools.partial(local, nx, ny), mesh=mesh, in_specs=in_specs, out_specs=out_specs, check_vma=False
    )
```

time: 203 us -> 86 us (0.42)
  waiting for transfers between devices: 133 us -> 0 us
  Pallas kernels: 0 us -> 83.5 us
  starting transfers between devices: 19.9 us -> 0 us
  local copies, waits for them, and re-layouts: 22.1 us -> 2.31 us
  between operations: 13.6 us -> 0.01 us
  matrix products: 8.13 us -> 0 us
  other arithmetic: 6.28 us -> 0 us
    pallas_call x0 -> x1, Pallas kernels: none -> 83.5 us  [local(): pl.pallas_call(functools.partial(kernel, nx, ny), out_shape=jax.ShapeDtyp...]
    all_to_all x2 -> x0, waiting for transfers between devices: 74.2 us -> none  [the longest x1 72.1 us: local(): lax.all_to_all(send_rows.reshape(owners, capacity, width), 'vocab', split...]
    reduce_scatter x1 -> x0, waiting for transfers between devices: 58.5 us -> none  [local(): lax.psum_scatter(jnp.dot(picker, got_rows, preferred_element_type=jnp.flo...]
    all_to_all x2 -> x0, starting transfers between devices: 19.8 us -> none  [the longest x1 11.6 us: local(): lax.all_to_all(send_cols.reshape(owners, capacity), 'vocab', split_axis=0...]
    gather x2 -> x0, local copies, waits for them, and re-layouts: 14.6 us -> none  [the longest x1 9.48 us: local(): send_cols = jnp.where(filled > 0, column[source], -1)]
    dot_general x1 -> x0, matrix products: 8.13 us -> none  [local(): jnp.dot(picker, got_rows, preferred_element_type=jnp.float32)]
    scatter x2 -> x0, local copies, waits for them, and re-layouts: 4.9 us -> none  [the longest x1 2.45 us: local(): source = jnp.zeros((owners * capacity,), jnp.int32).at[slot_index].set(jn...]
    convert_element_type x3 -> x0, other arithmetic: 2.15 us -> none  [the longest x1 2.13 us: local(): return lax.psum_scatter(jnp.dot(picker, got_rows, preferred_element_type=...]
  transfers between devices with their start and end apart: 3 -> 0, of which waited for: 3 -> 0; matrix products, arithmetic and copies ran while one was open for 4% -> 0% of each run, Pallas kernels for 0% -> 0%
where the time goes in v2:
time: 86 us; the launch traced here: 85.8 us
  Pallas kernels  83.5 us (97%)
  local copies, waits for them, and re-layouts  2.31 us (3%)
    pallas_call x1, Pallas kernels, local(): pl.pallas_call(functools.partial(kernel, nx, ny), out_shape=jax.ShapeDtyp...  83.5 us
    unnamed x1, local copies, waits for them, and re-layouts  2.31 us

profile of v2, /device:TPU:1, one launch (start us, length us, event | category | flops | bytes accessed | tf_op | source)
XLA Modules:
  0.0 85.8 jit_solution(18287331604449010017)
XLA Ops:
  0.0 83.5 %shard_map.28 = f32[256,1024]{1,0:T(8,128)} custom-call(bf16[32,1024]{1,0:T(8,128)(2,1)} %x_hbm.1, s32[16,32]{1,0:T(8,128)} %bitcast.1), custom_call_target="tpu_custom_call" | custom-call | tf_op jit(solution)/shard_map/pallas_call | solution.py:312
  83.5 2.3 %copy.4 = f32[256,1024]{1,0:T(8,128)} copy(f32[256,1024]{1,0:T(8,128)} %shard_map.28) | data formatting | bytes 2097152

commit v3 on v2

--- a/solution.py
+++ b/solution.py
@@ -21,9 +21,9 @@
 GROUPS = ((0, 3), (3, 5), (5, 8), (3, 8), (0, 8))
 
 
-def kernel(nx, ny, x_hbm, ids_hbm, out_hbm, x_in, ids_in, ids_x, ids_g, cnt, *rest):
-    xg, part, send, got, outs = (rest[NC * i : NC * (i + 1)] for i in range(5))
-    in_sem, out_sem, id_s, id_r, g_s, g_r, z_s, z_r = rest[5 * NC :]
+def kernel(nx, ny, x_hbm, ids_hbm, out_ref, x_in, ids_in, ids_x, ids_g, cnt, *rest):
+    xg, part, send, got = (rest[NC * i : NC * (i + 1)] for i in range(4))
+    in_sem, id_s, id_r, g_s, g_r, z_s, z_r = rest[4 * NC :]
     scope = jax.named_scope
     d = lax.axis_index("dp")
     v = lax.axis_index("vocab")
@@ -67,32 +67,30 @@
         for cp in copies:
             cp.start()
 
-    def whole(ref, sems, at_):
-        return rc(ref, ref, sems[0].at[*at_], sems[1].at[*at_], partner)
-
-    gs = (g_s, g_r)
+    def whole(ref, i):
+        return rc(ref, ref, id_s.at[i], id_r.at[i], partner)
 
     def along_y(f):
         src = x_in.at[:, pl.ds(OFFS[f], WIDTHS[f])]
         return [
-            rc(src, xg[f].at[c, y, x], g_s.at[f, 0], g_r.at[f, 0], at(x, ys[k], c)) for k in range(1, ny)
+            rc(src, xg[f].at[c, y, x], g_s.at[0], g_r.at[f, 0], at(x, ys[k], c)) for k in range(1, ny)
         ]
 
     def along_x(f):
         ref = xg[f].at[c, :, x]
-        return [rc(ref, ref, g_s.at[f, 1], g_r.at[f, 1], at(xs[k], y, c)) for k in (1, nx - 1)]
+        return [rc(ref, ref, g_s.at[1], g_r.at[f, 1], at(xs[k], y, c)) for k in (1, nx - 1)]
 
     def relay(f):
         lo = xg[f].at[c, pl.ds(0, ny // 2), xs[nx - 1]]
         hi = xg[f].at[c, pl.ds(ny // 2, ny // 2), xs[1]]
         return [
-            rc(lo, lo, g_s.at[f, 2], g_r.at[f, 2], at(xs[1], y, c)),
-            rc(hi, hi, g_s.at[f, 2], g_r.at[f, 2], at(xs[nx - 1], y, c)),
+            rc(lo, lo, g_s.at[2], g_r.at[f, 2], at(xs[1], y, c)),
+            rc(hi, hi, g_s.at[2], g_r.at[f, 2], at(xs[nx - 1], y, c)),
         ]
 
     def across(f, k):
         ref = xg[f].at[c, :, xs[k]]
-        return rc(ref, ref, g_s.at[f, 3], g_r.at[f, 3], partner)
+        return rc(ref, ref, g_s.at[3], g_r.at[f, 3], partner)
 
     def all_of(f, step):
         ref = (
@@ -101,7 +99,7 @@
             xg[f].at[c, :, 0],
             xg[f].at[c],
         )[step]
-        return whole(ref, gs, (f, step))
+        return rc(ref, ref, g_s.at[step], g_r.at[f, step], partner)
 
     def gather1(f):
         start(along_y(f))
@@ -131,8 +129,8 @@
     id1 = [rc(ids_x.at[x], ids_x.at[x], id_s.at[0], id_r.at[0], at(xs[k], y, c)) for k in range(1, nx)]
     id2 = [rc(ids_g.at[c, y], ids_g.at[c, y], id_s.at[1], id_r.at[1], at(x, ys[k], c)) for k in range(1, ny)]
     id3 = rc(ids_g.at[c], ids_g.at[c], id_s.at[2], id_r.at[2], partner)
-    id1_all = whole(ids_x.at[pl.ds(0, nx - 1)], (id_s, id_r), (0,))
-    id2_all = whole(ids_g.at[c, pl.ds(0, ny - 1)], (id_s, id_r), (1,))
+    id1_all = whole(ids_x.at[pl.ds(0, nx - 1)], 0)
+    id2_all = whole(ids_g.at[c, pl.ds(0, ny - 1)], 1)
 
     blocks = [lax.rem(d + k, 8) for k in BLOCKS]
     kt = 2 * ny
@@ -160,7 +158,7 @@
                 both = ((a & nib) + (b & nib), ((a >> 4) & nib) + ((b >> 4) & nib))
                 for s in range(8):
                     count = (both[s % 2] >> (8 * (s // 2))) & 255
-                    cnt[lo + n, pl.ds(32 * s, 32), pl.ds(pl.multiple_of(t * 128, 128), 128)] = count.astype(
+                    cnt[pl.ds(ROWS * (lo + n) + 32 * s, 32), pl.ds(pl.multiple_of(t * 128, 128), 128)] = count.astype(
                         jnp.float32
                     ).astype(jnp.bfloat16)
             return 0
@@ -168,18 +166,25 @@
         with scope(f"build{g}"):
             lax.fori_loop(0, ny, tile, 0)
 
+    once = jnp.minimum(d + 1, 1)
+
     def dots(f, g):
         lo, hi = GROUPS[g]
-        with scope(f"dot{f}{g}"):
+
+        def body(_, carry):
             part[f][lo:hi] = jnp.dot(
-                cnt[lo:hi].reshape((hi - lo) * ROWS, kt * 128),
+                cnt[ROWS * lo : ROWS * hi],
                 xg[f][...].reshape(kt * 128, WIDTHS[f]),
                 preferred_element_type=jnp.float32,
             ).reshape(hi - lo, ROWS, WIDTHS[f])
+            return carry
+
+        with scope(f"dot{f}{g}"):
+            lax.fori_loop(0, once, body, 0)
 
     def zcopy(way, f, m):
         return rc(
-            send[f].at[way, m], got[f].at[way, m], z_s.at[f], z_r.at[f, way, m], (down, up)[way]
+            send[f].at[way, m], got[f].at[way, m], z_s.at[0], z_r.at[f, way, m], (down, up)[way]
         )
 
     def reduce(f, r):
@@ -196,9 +201,6 @@
                 send[f][way, m] = value.astype(jnp.bfloat16)
                 zcopy(way, f, m).start()
 
-    def put(f):
-        return pltpu.make_async_copy(outs[f], out_hbm.at[:, pl.ds(OFFS[f], WIDTHS[f])], out_sem.at[f])
-
     def finish(f):
         with scope(f"fin{f}"):
             for m in (5, 6):
@@ -209,11 +211,11 @@
             total = part[f][7, rows] + (
                 got[f][0, 6 - half].astype(jnp.float32) + got[f][1, 5 + half].astype(jnp.float32)
             )
-            outs[f][rows] = total * (1.0 / LIST)
-        put(f).start()
+            out_ref[rows, OFFS[f] : OFFS[f] + WIDTHS[f]] = total * (1.0 / LIST)
 
     start(id1)
     gather1(0)
+    gather1(1)
     with scope("id1"):
         id1_all.wait_recv()
     lane = lax.broadcasted_iota(jnp.int32, (LIST, 128), 1) // POS
@@ -222,86 +224,86 @@
         both = jnp.where(lane == k, ids_x[k], both)
     ids_g[c, y] = both
     start(id2)
-    gather1(1)
+    gather1(2)
     gather2(0)
+    gather2(1)
     with scope("id2"):
         id2_all.wait_recv()
     id3.start()
+    gather3(0)
     build(0, c)
-    gather3(0)
     with scope("id3"):
         id3.wait_recv()
     build(0, 1 - c)
-    gather2(1)
-    gather1(2)
+    gather3(1)
+    gather2(2)
+    gather1(3)
+    gather1(4)
     build(1, c)
     gather4(0)
     build(1, 1 - c)
     gather5(0)
     dots(0, 0)
     reduce(0, 0)
-    gather3(1)
+    build(2, c)
     dots(0, 1)
-    build(2, c)
-    gather2(2)
-    gather1(3)
-    build(2, 1 - c)
     gather4(1)
-    reduce(0, 1)
     gather5(1)
     dots(1, 0)
+    reduce(0, 1)
     reduce(1, 0)
     gather3(2)
+    gather2(3)
+    build(2, 1 - c)
     dots(0, 2)
+    dots(1, 3)
     reduce(0, 2)
-    dots(1, 3)
     gather4(2)
-    gather2(3)
-    gather1(4)
     reduce(1, 1)
+    gather3(3)
+    gather2(4)
     gather5(2)
     dots(2, 0)
     reduce(2, 0)
     reduce(0, 3)
     dots(2, 3)
-    gather3(3)
     reduce(1, 2)
+    gather3(4)
+    gather4(3)
     reduce(2, 1)
-    gather2(4)
-    finish(0)
-    gather4(3)
     gather5(3)
-    dots(3, 0)
+    dots(3, 4)
     reduce(3, 0)
-    reduce(1, 3)
-    dots(3, 3)
-    reduce(2, 2)
-    gather3(4)
-    reduce(3, 1)
-    finish(1)
     gather4(4)
     gather5(4)
     dots(4, 4)
     reduce(4, 0)
+    finish(0)
+    reduce(1, 3)
+    reduce(2, 2)
+    reduce(3, 1)
+    reduce(4, 1)
+    finish(1)
     reduce(2, 3)
     reduce(3, 2)
-    reduce(4, 1)
+    reduce(4, 2)
     finish(2)
     reduce(3, 3)
-    reduce(4, 2)
+    reduce(4, 3)
     finish(3)
-    reduce(4, 3)
     finish(4)
 
     with scope("drain"):
         id1_all.wait_send()
         id2_all.wait_send()
         id3.wait_send()
-        for f in range(NC):
-            for step in range(4):
-                all_of(f, step).wait_send()
-            rc(send[f], send[f], z_s.at[f], z_r.at[f, 0, 0], down).wait_send()
-            put(f).wait()
+        width = x_in.shape[1]
+        depth = kt * 128
+        for step, rows in enumerate(((ny - 1) * POS, 2 * ny * POS, ny * POS, nx * ny * POS)):
+            ref = cnt.at[pl.ds(0, rows * width // depth)]
+            rc(ref, ref, g_s.at[step], g_r.at[0, step], partner).wait_send()
+        ref = cnt.at[pl.ds(0, 14 * HALF * width // depth)]
+        rc(ref, ref, z_s.at[0], z_r.at[0, 0, 0], down).wait_send()
 
 
 def local(nx, ny, pooled_grad, token_ids):
@@ -313,20 +315,19 @@
         functools.partial(kernel, nx, ny),
         out_shape=jax.ShapeDtypeStruct((ROWS, width), jnp.float32),
         in_specs=[pl.BlockSpec(memory_space=pl.ANY)] * 2,
-        out_specs=pl.BlockSpec(memory_space=pl.ANY),
+        out_specs=pl.BlockSpec(memory_space=pltpu.VMEM),
         scratch_shapes=[
             vmem((POS, width), bf),
             vmem((LIST, POS), jnp.int32),
             vmem((nx, LIST, 128), jnp.int32),
             vmem((2, ny, LIST, 128), jnp.int32),
-            vmem((8, ROWS, 2 * ny * 128), bf),
+            vmem((8 * ROWS, 2 * ny * 128), bf),
             *[vmem((2, ny, nx, POS, w), bf) for w in WIDTHS],
             *[vmem((8, ROWS, w), jnp.float32) for w in WIDTHS],
             *[vmem((2, 7, HALF, w), bf) for w in WIDTHS],
             *[vmem((2, 7, HALF, w), bf) for w in WIDTHS],
-            *[vmem((ROWS, w), jnp.float32) for w in WIDTHS],
-            dma((2,)), dma((NC,)), dma((3,)), dma((3,)),
-            dma((NC, 4)), dma((NC, 4)), dma((NC,)), dma((NC, 2, 7)),
+            dma((2,)), dma((3,)), dma((3,)),
+            dma((4,)), dma((NC, 4)), dma((1,)), dma((NC, 2, 7)),
         ],
         compiler_params=pltpu.CompilerParams(
             collective_id=0, has_side_effects=True, vmem_limit_bytes=62 * 1024 * 1024

time: 86 us -> 80.2 us (0.933)
  Pallas kernels: 83.5 us -> 77.7 us
    pallas_call x1, Pallas kernels: 83.5 us -> 77.7 us  [local(): pl.pallas_call(functools.partial(kernel, nx, ny), out_shape=jax.ShapeDtyp...]
where the time goes in v3:
time: 80.2 us; the launch traced here: 80 us
  Pallas kernels  77.7 us (97%)
  local copies, waits for them, and re-layouts  2.31 us (3%)
    pallas_call x1, Pallas kernels, local(): pl.pallas_call(functools.partial(kernel, nx, ny), out_shape=jax.ShapeDtyp...  77.7 us
    unnamed x1, local copies, waits for them, and re-layouts  2.31 us

profile of v3, /device:TPU:1, one launch (start us, length us, event | category | flops | bytes accessed | tf_op | source)
XLA Modules:
  0.0 80.0 jit_solution(1824419549958909590)
XLA Ops:
  0.0 77.7 %shard_map.28 = f32[256,1024]{1,0:T(8,128)} custom-call(bf16[32,1024]{1,0:T(8,128)(2,1)} %x_hbm.1, s32[16,32]{1,0:T(8,128)} %bitcast.1), custom_call_target="tpu_custom_call" | custom-call | tf_op jit(solution)/shard_map/pallas_call | solution.py:314
  77.7 2.3 %copy.4 = f32[256,1024]{1,0:T(8,128)} copy(f32[256,1024]{1,0:T(8,128)} %shard_map.28) | data formatting | bytes 2097152

commit v4 on v3

v4 whole, which is shorter than its diff:
```python
import functools

import jax
import jax.numpy as jnp
from jax import lax
from jax.experimental import pallas as pl
from jax.experimental.pallas import tpu as pltpu
from jax.sharding import PartitionSpec as P

ROWS = 256
HALF = ROWS // 2
LIST = 16
POS = 32
WIDTHS = (128, 256, 256, 256, 128)
OFFS = tuple(sum(WIDTHS[:i]) for i in range(len(WIDTHS)))
NC = len(WIDTHS)
MESH = pl.DeviceIdType.MESH
MSG = ((3, 0), (3, 1), (2, 0), (2, 1), (1, 0), (1, 1))
ROUNDS = ((0, 1), (2, 3), (4, 5))
BLOCKS = (0, 5, 3, 6, 2, 7, 1, 0)
FAR, A, B, C, BC, ABC = (0, 1), (1, 3), (3, 5), (5, 8), (3, 8), (1, 8)


def kernel(nx, ny, x_hbm, ids_hbm, out_ref, x_in, x_far, ids_in, ids_far, ids_x, ids_g, cnt, *rest):
    part, send, got = (rest[NC * i : NC * (i + 1)] for i in range(3))
    xg = rest[3 * NC : 5 * NC]
    in_sem, id_s, id_r, g_s, g_r, z_s, z_r = rest[5 * NC :]
    scope = jax.named_scope
    d = lax.axis_index("dp")
    v = lax.axis_index("vocab")
    c = v % 2
    y = (v // 2) % ny
    x = v // (2 * ny)

    def at(xx, yy, cc):
        return (d, (xx * ny + yy) * 2 + cc)

    far_first = [sorted(range(1, n), key=lambda k, n=n: -min(k, n - k)) for n in (nx, ny)]
    xs = [lax.rem(x + k, nx) for k in range(nx)]
    ys = [lax.rem(y + k, ny) for k in range(ny)]
    partner = at(x, y, 1 - c)
    down = (lax.rem(d + 7, 8), v)
    up = (lax.rem(d + 1, 8), v)
    far = (lax.rem(d + 4, 8), v)

    cp_ids = pltpu.make_async_copy(ids_hbm, ids_in, in_sem.at[0])
    cp_x = pltpu.make_async_copy(x_hbm, x_in, in_sem.at[1])
    cp_ids.start()
    cp_x.start()

    peers = [at(x, ys[k], c) for k in range(1, ny)] + [at(xs[k], y, c) for k in range(1, nx)]
    peers += [partner, down, up, far]
    barrier = pltpu.get_barrier_semaphore()
    for peer in peers:
        pl.semaphore_signal(barrier, inc=1, device_id=peer, device_id_type=MESH)
    cp_ids.wait()
    ids_x[0, x] = jnp.concatenate([ids_in[...]] * nx, axis=1)
    cp_x.wait()
    for f in range(NC):
        xg[f][c, y, x] = x_in[:, pl.ds(OFFS[f], WIDTHS[f])]
    with scope("barrier"):
        pl.semaphore_wait(barrier, len(peers))

    def rc(src, dst, ss, rs, dev):
        return pltpu.make_async_remote_copy(
            src_ref=src, dst_ref=dst, send_sem=ss, recv_sem=rs, device_id=dev, device_id_type=MESH
        )

    def start(copies):
        for cp in copies:
            cp.start()

    def whole(ref, i):
        return rc(ref, ref, id_s.at[i], id_r.at[i], partner)

    def along_y(f):
        src = (x_in if f < NC else x_far).at[:, pl.ds(OFFS[f % NC], WIDTHS[f % NC])]
        return [
            rc(src, xg[f].at[c, y, x], g_s.at[0], g_r.at[f, 0], at(x, ys[k], c)) for k in far_first[1]
        ]

    def along_x(f):
        ref = xg[f].at[c, :, x]
        return [rc(ref, ref, g_s.at[1], g_r.at[f, 1], at(xs[k], y, c)) for k in (1, nx - 1)]

    def relay(f):
        lo = xg[f].at[c, pl.ds(0, ny // 2), xs[nx - 1]]
        hi = xg[f].at[c, pl.ds(ny // 2, ny // 2), xs[1]]
        return [
            rc(lo, lo, g_s.at[2], g_r.at[f, 2], at(xs[1], y, c)),
            rc(hi, hi, g_s.at[2], g_r.at[f, 2], at(xs[nx - 1], y, c)),
        ]

    def across(f, k):
        ref = xg[f].at[c, :, xs[k]]
        return rc(ref, ref, g_s.at[3], g_r.at[f, 3], partner)

    def all_of(f, step):
        ref = (
            xg[f].at[c, pl.ds(0, ny - 1), 0],
            xg[f].at[c, :, pl.ds(0, 2)],
            xg[f].at[c, :, 0],
            xg[f].at[c],
        )[step]
        return rc(ref, ref, g_s.at[step], g_r.at[f, step], partner)

    def gather1(f):
        start(along_y(f))

    def gather2(f):
        with scope(f"g2_{f}"):
            all_of(f, 0).wait_recv()
        start(along_x(f))
        across(f, 0).start()

    def gather3(f):
        with scope(f"g3_{f}"):
            all_of(f, 1).wait_recv()
        start(relay(f))
        across(f, 1).start()
        across(f, nx - 1).start()

    def gather4(f):
        with scope(f"g4_{f}"):
            all_of(f, 2).wait_recv()
        across(f, 2).start()

    def gather5(f):
        with scope(f"g5_{f}"):
            all_of(f, 3).wait_recv()

    def ids_copies(e):
        near = ids_x.at[e, x]
        line = ids_g.at[e, c, y]
        plane = ids_g.at[e, c]
        k = 3 * e
        return (
            [rc(near, near, id_s.at[k], id_r.at[k], at(xs[i], y, c)) for i in far_first[0]],
            [rc(line, line, id_s.at[k + 1], id_r.at[k + 1], at(x, ys[i], c)) for i in far_first[1]],
            [rc(plane, plane, id_s.at[k + 2], id_r.at[k + 2], partner)],
            whole(ids_x.at[e, pl.ds(0, nx - 1)], k),
            whole(ids_g.at[e, c, pl.ds(0, ny - 1)], k + 1),
            whole(plane, k + 2),
        )

    ids_near, ids_away = ids_copies(0), ids_copies(1)

    def join(e):
        lane = lax.broadcasted_iota(jnp.int32, (LIST, 128), 1) // POS
        both = ids_x[e, 0]
        for k in range(1, nx):
            both = jnp.where(lane == k, ids_x[e, k], both)
        ids_g[e, c, y] = both

    to_far = (
        rc(ids_x.at[0, x], ids_far, id_s.at[6], id_r.at[6], far),
        rc(x_in, x_far, id_s.at[7], id_r.at[7], far),
    )

    blocks = [lax.rem(d + k, 8) for k in BLOCKS]
    kt = 2 * ny

    def build(g, core, e=0):
        lo, hi = g

        def tile(k, _):
            ids = ids_g[e, core, k]
            t = core * ny + k
            low = ids & (ROWS - 1)
            block = ids >> 8
            word = low & 31
            bit = jnp.left_shift(1, (low >> 5) * 4)
            wide = lax.broadcasted_iota(jnp.int32, (32, 128), 0)
            vals = [jnp.where(block == blocks[i] * (2 * nx * ny) + v, bit, 0) for i in range(lo, hi)]
            acc = [[jnp.zeros((32, 128), jnp.int32) for _ in range(2)] for _ in vals]
            for j in range(LIST):
                eq = jnp.broadcast_to(word[j : j + 1], (32, 128)) == wide
                for n, val in enumerate(vals):
                    acc[n][j // 8] += jnp.where(eq, jnp.broadcast_to(val[j : j + 1], (32, 128)), 0)
            nib = 0x0F0F0F0F
            for n in range(len(vals)):
                a, b = acc[n]
                both = ((a & nib) + (b & nib), ((a >> 4) & nib) + ((b >> 4) & nib))
                for s in range(8):
                    count = (both[s % 2] >> (8 * (s // 2))) & 255
                    cnt[pl.ds(ROWS * (lo + n) + 32 * s, 32), pl.ds(pl.multiple_of(t * 128, 128), 128)] = count.astype(
                        jnp.float32
                    ).astype(jnp.bfloat16)
            return 0

        with scope(f"build{lo}"):
            lax.fori_loop(0, ny, tile, 0)

    once = jnp.minimum(d + 1, 1)

    def dots(f, g):
        lo, hi = g
        rows = xg[f + NC] if g is FAR else xg[f]

        def body(_, carry):
            part[f][lo:hi] = jnp.dot(
                cnt[ROWS * lo : ROWS * hi],
                rows[...].reshape(kt * 128, WIDTHS[f]),
                preferred_element_type=jnp.float32,
            ).reshape(hi - lo, ROWS, WIDTHS[f])
            return carry

        with scope(f"dot{f}{lo}"):
            lax.fori_loop(0, once, body, 0)

    def zcopy(way, f, m):
        return rc(
            send[f].at[way, m], got[f].at[way, m], z_s.at[0], z_r.at[f, m], (down, up)[way]
        )

    def zwait(f, m):
        ref = got[f].at[:, m]
        with scope(f"w{f}{m}"):
            rc(ref, ref, z_s.at[0], z_r.at[f, m], down).wait_recv()

    def reduce(f, r, some=(0, 1)):
        for m in (ROUNDS[r][i] for i in some):
            dist, half = MSG[m]
            if m >= 2:
                zwait(f, m - 2)
            for way in range(2):
                i = 2 * (4 - dist) - 1 + way
                value = part[f][i, HALF * half : HALF * (half + 1)]
                if m >= 2:
                    value = value + got[f][way, m - 2].astype(jnp.float32)
                send[f][way, m] = value.astype(jnp.bfloat16)
                zcopy(way, f, m).start()

    def finish(f):
        gather5(f + NC)
        dots(f, FAR)
        for half in range(2):
            zwait(f, 4 + half)
            rows = slice(HALF * half, HALF * (half + 1))
            total = (part[f][7, rows] + part[f][0, rows]) + (
                got[f][0, 4 + half].astype(jnp.float32) + got[f][1, 4 + half].astype(jnp.float32)
            )
            out_ref[rows, OFFS[f] : OFFS[f] + WIDTHS[f]] = total * (1.0 / LIST)

    start(ids_near[0])
    gather1(0)
    gather1(1)
    start(to_far)
    with scope("id1"):
        ids_near[3].wait_recv()
    join(0)
    start(ids_near[1])
    gather1(2)
    gather2(0)
    gather2(1)
    with scope("id2"):
        ids_near[4].wait_recv()
    start(ids_near[2])
    gather3(0)
    build(A, c)
    with scope("id3"):
        ids_near[5].wait_recv()
    build(A, 1 - c)
    gather3(1)
    gather2(2)
    gather1(3)
    gather1(4)
    to_far[0].wait_recv()
    ids_x[1, x] = ids_far[...]
    start(ids_away[0])
    build(B, c)
    gather4(0)
    build(B, 1 - c)
    gather5(0)
    dots(0, A)
    reduce(0, 0)
    to_far[1].wait_recv()
    for f in range(NC):
        xg[NC + f][c, y, x] = x_far[:, pl.ds(OFFS[f], WIDTHS[f])]
        gather1(NC + f)
    build(C, c)
    dots(0, B)
    gather4(1)
    gather5(1)
    dots(1, A)
    reduce(0, 1)
    reduce(1, 0)
    gather3(2)
    gather2(3)
    with scope("far"):
        ids_away[3].wait_recv()
    join(1)
    start(ids_away[1])
    build(C, 1 - c)
    dots(0, C)
    dots(1, BC)
    reduce(0, 2)
    gather4(2)
    reduce(1, 1)
    gather3(3)
    gather2(4)
    gather2(5)
    gather5(2)
    dots(2, A)
    reduce(2, 0)
    dots(2, BC)
    with scope("id2far"):
        ids_away[4].wait_recv()
    start(ids_away[2])
    reduce(1, 2)
    gather3(4)
    gather4(3)
    gather2(6)
    gather3(5)
    reduce(2, 1)
    gather2(7)
    gather5(3)
    dots(3, ABC)
    reduce(3, 0)
    gather4(4)
    gather5(4)
    gather2(8)
    dots(4, ABC)
    reduce(4, 0)
    gather4(5)
    gather3(6)
    gather2(9)
    reduce(2, 2)
    ids_away[5].wait_recv()
    build(FAR, c, 1)
    build(FAR, 1 - c, 1)
    gather3(7)
    reduce(3, 1)
    reduce(4, 1)
    finish(0)
    gather4(6)
    gather3(8)
    reduce(3, 2, (0,))
    gather4(7)
    gather3(9)
    reduce(3, 2, (1,))
    finish(1)
    reduce(4, 2)
    gather4(8)
    finish(2)
    gather4(9)
    finish(3)
    finish(4)

    with scope("drain"):
        for copies in (ids_near, ids_away):
            for step in (3, 4, 5):
                copies[step].wait_send()
        for cp in to_far:
            cp.wait_send()
        width = x_in.shape[1]
        depth = kt * 128
        for step, rows in enumerate(((ny - 1) * POS, 2 * ny * POS, ny * POS, nx * ny * POS)):
            ref = cnt.at[pl.ds(0, 2 * rows * width // depth)]
            rc(ref, ref, g_s.at[step], g_r.at[0, step], partner).wait_send()
        ref = cnt.at[pl.ds(0, 2 * len(MSG) * HALF * width // depth)]
        rc(ref, ref, z_s.at[0], z_r.at[0, 0], down).wait_send()


def local(nx, ny, pooled_grad, token_ids):
    width = pooled_grad.shape[1]
    dma = pltpu.SemaphoreType.DMA
    bf = jnp.bfloat16
    vmem = pltpu.VMEM
    return pl.pallas_call(
        functools.partial(kernel, nx, ny),
        out_shape=jax.ShapeDtypeStruct((ROWS, width), jnp.float32),
        in_specs=[pl.BlockSpec(memory_space=pl.ANY)] * 2,
        out_specs=pl.BlockSpec(memory_space=pltpu.VMEM),
        scratch_shapes=[
            vmem((POS, width), bf),
            vmem((POS, width), bf),
            vmem((LIST, POS), jnp.int32),
            vmem((LIST, 128), jnp.int32),
            vmem((2, nx, LIST, 128), jnp.int32),
            vmem((2, 2, ny, LIST, 128), jnp.int32),
            vmem((8 * ROWS, 2 * ny * 128), bf),
            *[vmem((8, ROWS, w), jnp.float32) for w in WIDTHS],
            *[vmem((2, len(MSG), HALF, w), bf) for w in WIDTHS],
            *[vmem((2, len(MSG), HALF, w), bf) for w in WIDTHS],
            *[vmem((2, ny, nx, POS, w), bf) for w in WIDTHS + WIDTHS],
            dma((2,)), dma((8,)), dma((8,)),
            dma((4,)), dma((2 * NC, 4)), dma((1,)), dma((NC, len(MSG))),
        ],
        compiler_params=pltpu.CompilerParams(
            collective_id=0, has_side_effects=True, vmem_limit_bytes=62 * 1024 * 1024
        ),
    )(pooled_grad, token_ids.T)


def solution(mesh, nx=4, ny=8):
    in_specs = (P(("dp", "vocab"), None), P(("dp", "vocab"), None))
    out_specs = P(("dp", "vocab"), None)
    return jax.shard_map(
        functools.partial(local, nx, ny), mesh=mesh, in_specs=in_specs, out_specs=out_specs, check_vma=False
    )
```

time: 80.2 us -> 74.2 us (0.925)
  Pallas kernels: 77.7 us -> 71.7 us
    pallas_call x1, Pallas kernels: 77.7 us -> 71.7 us  [local(): pl.pallas_call(functools.partial(kernel, nx, ny), out_shape=jax.ShapeDtyp...]
where the time goes in v4:
time: 74.2 us; the launch traced here: 74 us
  Pallas kernels  71.7 us (97%)
  local copies, waits for them, and re-layouts  2.31 us (3%)
    pallas_call x1, Pallas kernels, local(): pl.pallas_call(functools.partial(kernel, nx, ny), out_shape=jax.ShapeDtyp...  71.7 us
    unnamed x1, local copies, waits for them, and re-layouts  2.31 us

profile of v4, /device:TPU:1, one launch (start us, length us, event | category | flops | bytes accessed | tf_op | source)
XLA Modules:
  0.0 74.0 jit_solution(5445208514019236799)
XLA Ops:
  0.0 71.7 %shard_map.28 = f32[256,1024]{1,0:T(8,128)} custom-call(bf16[32,1024]{1,0:T(8,128)(2,1)} %x_hbm.1, s32[16,32]{1,0:T(8,128)} %bitcast.1), custom_call_target="tpu_custom_call" | custom-call | tf_op jit(solution)/shard_map/pallas_call | solution.py:370
  71.7 2.3 %copy.4 = f32[256,1024]{1,0:T(8,128)} copy(f32[256,1024]{1,0:T(8,128)} %shard_map.28) | data formatting | bytes 2097152

commit v5 on v4

--- a/solution.py
+++ b/solution.py
@@ -279,71 +279,73 @@
         xg[NC + f][c, y, x] = x_far[:, pl.ds(OFFS[f], WIDTHS[f])]
         gather1(NC + f)
     build(C, c)
+    gather4(1)
     dots(0, B)
-    gather4(1)
     gather5(1)
     dots(1, A)
-    reduce(0, 1)
     reduce(1, 0)
     gather3(2)
     gather2(3)
+    reduce(0, 1)
     with scope("far"):
         ids_away[3].wait_recv()
     join(1)
     start(ids_away[1])
     build(C, 1 - c)
-    dots(0, C)
     dots(1, BC)
-    reduce(0, 2)
-    gather4(2)
     reduce(1, 1)
-    gather3(3)
     gather2(4)
     gather2(5)
+    gather4(2)
+    dots(0, C)
+    reduce(0, 2)
+    gather3(3)
     gather5(2)
     dots(2, A)
     reduce(2, 0)
     dots(2, BC)
+    reduce(1, 2)
+    gather2(6)
+    gather3(4)
+    reduce(2, 1, (0,))
+    gather3(5)
+    gather4(3)
+    reduce(2, 1, (1,))
+    gather2(7)
     with scope("id2far"):
         ids_away[4].wait_recv()
     start(ids_away[2])
-    reduce(1, 2)
-    gather3(4)
-    gather4(3)
-    gather2(6)
-    gather3(5)
-    reduce(2, 1)
-    gather2(7)
     gather5(3)
     dots(3, ABC)
     reduce(3, 0)
+    gather3(6)
+    gather2(8)
     gather4(4)
+    gather4(5)
+    reduce(2, 2, (0,))
     gather5(4)
-    gather2(8)
     dots(4, ABC)
     reduce(4, 0)
-    gather4(5)
-    gather3(6)
+    reduce(2, 2, (1,))
     gather2(9)
-    reduce(2, 2)
+    gather3(7)
     ids_away[5].wait_recv()
     build(FAR, c, 1)
     build(FAR, 1 - c, 1)
-    gather3(7)
     reduce(3, 1)
+    gather4(6)
     reduce(4, 1)
     finish(0)
-    gather4(6)
     gather3(8)
     reduce(3, 2, (0,))
-    gather4(7)
     gather3(9)
     reduce(3, 2, (1,))
-    finish(1)
+    gather4(7)
     reduce(4, 2)
     gather4(8)
+    finish(1)
+    gather4(9)
     finish(2)
-    gather4(9)
     finish(3)
     finish(4)
 

time: 74.2 us -> 72.3 us (0.974)
  Pallas kernels: 71.7 us -> 69.8 us
    pallas_call x1, Pallas kernels: 71.7 us -> 69.8 us  [local(): pl.pallas_call(functools.partial(kernel, nx, ny), out_shape=jax.ShapeDtyp...]
where the time goes in v5:
time: 72.3 us; the launch traced here: 72.1 us
  Pallas kernels  69.8 us (97%)
  local copies, waits for them, and re-layouts  2.31 us (3%)
    pallas_call x1, Pallas kernels, local(): pl.pallas_call(functools.partial(kernel, nx, ny), out_shape=jax.ShapeDtyp...  69.8 us
    unnamed x1, local copies, waits for them, and re-layouts  2.31 us

profile of v5, /device:TPU:1, one launch (start us, length us, event | category | flops | bytes accessed | tf_op | source)
XLA Modules:
  0.0 72.1 jit_solution(12138378231840642789)
XLA Ops:
  0.0 69.8 %shard_map.28 = f32[256,1024]{1,0:T(8,128)} custom-call(bf16[32,1024]{1,0:T(8,128)(2,1)} %x_hbm.1, s32[16,32]{1,0:T(8,128)} %bitcast.1), custom_call_target="tpu_custom_call" | custom-call | tf_op jit(solution)/shard_map/pallas_call | solution.py:372
  69.8 2.3 %copy.4 = f32[256,1024]{1,0:T(8,128)} copy(f32[256,1024]{1,0:T(8,128)} %shard_map.28) | data formatting | bytes 2097152

commit v6 on v5

--- a/solution.py
+++ b/solution.py
@@ -278,9 +278,8 @@
     for f in range(NC):
         xg[NC + f][c, y, x] = x_far[:, pl.ds(OFFS[f], WIDTHS[f])]
         gather1(NC + f)
-    build(C, c)
+    dots(0, B)
     gather4(1)
-    dots(0, B)
     gather5(1)
     dots(1, A)
     reduce(1, 0)
@@ -291,20 +290,23 @@
         ids_away[3].wait_recv()
     join(1)
     start(ids_away[1])
-    build(C, 1 - c)
-    dots(1, BC)
-    reduce(1, 1)
+    build(C, c)
+    dots(1, B)
+    reduce(1, 1, (0,))
+    gather4(2)
+    reduce(1, 1, (1,))
+    gather5(2)
+    dots(2, A)
+    reduce(2, 0)
     gather2(4)
     gather2(5)
-    gather4(2)
+    build(C, 1 - c)
     dots(0, C)
     reduce(0, 2)
     gather3(3)
-    gather5(2)
-    dots(2, A)
-    reduce(2, 0)
+    dots(1, C)
+    reduce(1, 2)
     dots(2, BC)
-    reduce(1, 2)
     gather2(6)
     gather3(4)
     reduce(2, 1, (0,))

time: 72.3 us -> 71.9 us (level)
  no operation moved by 1% of the time
where the time goes in v6:
time: 71.9 us; the launch traced here: 71.8 us
  Pallas kernels  69.4 us (97%)
  local copies, waits for them, and re-layouts  2.31 us (3%)
    pallas_call x1, Pallas kernels, local(): pl.pallas_call(functools.partial(kernel, nx, ny), out_shape=jax.ShapeDtyp...  69.4 us
    unnamed x1, local copies, waits for them, and re-layouts  2.31 us

profile of v6, /device:TPU:1, one launch (start us, length us, event | category | flops | bytes accessed | tf_op | source)
XLA Modules:
  0.0 71.8 jit_solution(15274219012206576145)
XLA Ops:
  0.0 69.4 %shard_map.28 = f32[256,1024]{1,0:T(8,128)} custom-call(bf16[32,1024]{1,0:T(8,128)(2,1)} %x_hbm.1, s32[16,32]{1,0:T(8,128)} %bitcast.1), custom_call_target="tpu_custom_call" | custom-call | tf_op jit(solution)/shard_map/pallas_call | solution.py:374
  69.4 2.3 %copy.4 = f32[256,1024]{1,0:T(8,128)} copy(f32[256,1024]{1,0:T(8,128)} %shard_map.28) | data formatting | bytes 2097152
